TPU v7x, 32 devices: a whole 2x2x4 slice. The times are simulated.
32 devices in a mesh: track: 16 (over z, y, x), cam: 2 (over core).
Axes of the slice: x: 2, y: 2, z: 4, core: 2. Of those that a mesh axis runs over, the one named last changes fastest.
Arguments:
- omega: bfloat16 [32, 9, 4096], P(None, None, ('track', 'cam')), may hold values from -6 to 6
- u_blocks: float32 [9, 9, 4096], P(None, None, ('track', 'cam')), may hold values from -5.4 to 36, as said below
- w_blocks: bfloat16 [9, 3, 16384], P(None, None, ('track', 'cam')), may hold values from -1.796875 to 1.796875
- v_inverse: float32 [3, 3, 4096], P(None, None, ('track', 'cam')), may hold values from -0.6 to 1.5, as said below
- obs_camera: int32 [16384], P(('track', 'cam')), may hold values from 0 to 4095, as said below
- obs_track: int32 [16384], P(('track', 'cam')), may hold values from 0 to 31, as said below
- obs_mask: int32 [16384], P(('track', 'cam')), may hold values from 0 to 1, as said below
Outputs:
- sketch: float32 [32, 9, 4096], P(None, None, ('track', 'cam'))
- basis: float32 [32, 9, 4096], P(None, None, ('track', 'cam'))
- factor: float32 [32, 32], replicated
Inputs may be any that keep to these rules, and one draw needn't show every extreme that they name: `obs_camera`: cameras c * 128 to (c + 1) * 128 - 1 belong to device c (track slower). Among one device's 512 observations, padding included, at most 32 name cameras of any one device, and exactly 32 name those of some device. `obs_track`: in each aligned block of 128 observations, slots 0 to 31 each hold one track of 2 to 4 consecutive observations from the block's start, in rising order; the padding after them carries slot 31. `obs_mask`: 1 on the observations of tracks, 0 on the padding at the end of each block. `u_blocks`: each block is symmetric. `v_inverse`: each block is symmetric positive definite.
All inputs are finite; a program needn't handle non-finite values.
Results may differ from a plain program's by a relative error of at most 0.00095.
Values may be sent and summed in bfloat16 or wider, within the bound.
A program may use at most 64 MiB of HBM per device.

v0:
```python
import jax
import jax.numpy as jnp
from jax import lax
from jax.sharding import PartitionSpec as P

BLK_OBS = 128
TRK_BLK = 32
HIGH = lax.Precision.HIGHEST


def eliminate(gathered, w_blocks, v_inverse, obs_track, obs_mask):
    weights = w_blocks.astype(jnp.float32)
    live_mask = obs_mask.astype(jnp.float32)
    values = gathered.astype(jnp.float32)
    columns = values.shape[1]
    obs_count = values.shape[2]
    blocks = obs_count // BLK_OBS
    projected = (
        jnp.stack(
            [
                sum(
                    (
                        weights[comp_row, comp_col][None, :] * values[comp_row]
                        for comp_row in range(9)
                    )
                )
                for comp_col in range(3)
            ]
        )
        * live_mask
    )
    member = (
        obs_track.reshape(blocks, BLK_OBS)[:, :, None] == jnp.arange(TRK_BLK, dtype=jnp.int32)
    ).astype(jnp.float32)
    summed = jnp.einsum(
        "icbo,bot->icbt", projected.reshape(3, columns, blocks, BLK_OBS), member, precision=HIGH
    ).reshape(3, columns, blocks * TRK_BLK)
    solved = jnp.stack(
        [
            sum(
                (v_inverse[comp_row, comp_col][None, :] * summed[comp_col] for comp_col in range(3))
            )
            for comp_row in range(3)
        ]
    )
    spread = jnp.einsum(
        "icbt,bot->icbo", solved.reshape(3, columns, blocks, TRK_BLK), member, precision=HIGH
    ).reshape(3, columns, obs_count)
    returned = (
        jnp.stack(
            [
                sum(
                    (
                        weights[comp_row, comp_col][None, :] * spread[comp_col]
                        for comp_col in range(3)
                    )
                )
                for comp_row in range(9)
            ]
        )
        * live_mask
    )
    return returned.astype(jnp.bfloat16)


def on_device(omega, u_blocks, w_blocks, v_inverse, obs_camera, obs_track, obs_mask):
    track_count = lax.axis_size("track")
    cam_count = lax.axis_size("cam")
    devices = track_count * cam_count
    columns, params, cam_width = omega.shape
    obs_count = obs_camera.shape[0]
    capacity = max(2, 2 * obs_count // devices)
    buffer_slots = devices * capacity
    owner_index = obs_camera // cam_width
    ordering = jnp.argsort(owner_index, stable=True)
    ranked = owner_index[ordering]
    first_index = jnp.searchsorted(ranked, ranked, side="left")
    placed = ranked * capacity + jnp.arange(obs_count, dtype=jnp.int32) - first_index
    slot_index = jnp.zeros((obs_count,), jnp.int32).at[ordering].set(placed)
    request = (
        jnp.full((buffer_slots,), -1, jnp.int32)
        .at[slot_index]
        .set(obs_camera)
        .reshape(track_count, cam_count, capacity)
    )
    camera_ids = lax.all_to_all(
        lax.all_to_all(request, "track", split_axis=0, concat_axis=0, tiled=True),
        "cam",
        split_axis=1,
        concat_axis=1,
        tiled=True,
    )
    table_start = (lax.axis_index("track") * cam_count + lax.axis_index("cam")) * cam_width
    table_width = omega.shape[2]
    is_live = camera_ids >= 0
    local_ids = jnp.where(is_live, camera_ids - table_start, 0).reshape(-1)
    gathered_rows = jnp.take(omega, local_ids, axis=2)
    outgoing = (
        gathered_rows.reshape(columns, params, track_count, cam_count, capacity)
        .transpose(2, 3, 1, 4, 0)
        .reshape(track_count, cam_count, params, capacity * columns)
    )
    returned = lax.all_to_all(
        lax.all_to_all(outgoing, "track", split_axis=0, concat_axis=0, tiled=True),
        "cam",
        split_axis=1,
        concat_axis=1,
        tiled=True,
    )
    received = (
        returned.reshape(track_count, cam_count, params, capacity, columns)
        .transpose(2, 4, 0, 1, 3)
        .reshape(params, columns, buffer_slots)
    )
    needed = jnp.take(received, slot_index, axis=2)
    contribution = eliminate(needed, w_blocks, v_inverse, obs_track, obs_mask)
    buffer = (
        jnp.zeros((params, columns, buffer_slots), jnp.bfloat16)
        .at[:, :, slot_index]
        .set(contribution)
    )
    packed = (
        buffer.reshape(params, columns, track_count, cam_count, capacity)
        .transpose(2, 3, 0, 4, 1)
        .reshape(track_count, cam_count, params, capacity * columns)
    )
    arrived = lax.all_to_all(
        lax.all_to_all(packed, "track", split_axis=0, concat_axis=0, tiled=True),
        "cam",
        split_axis=1,
        concat_axis=1,
        tiled=True,
    )
    terms = (
        arrived.reshape(track_count, cam_count, params, capacity, columns)
        .transpose(4, 2, 0, 1, 3)
        .reshape(columns, params, buffer_slots)
        .astype(jnp.float32)
    )
    target = jnp.where(is_live, camera_ids - table_start, table_width).reshape(-1)
    incoming = (
        jnp.zeros((columns, params, table_width + 1), jnp.float32)
        .at[:, :, target]
        .add(terms)[:, :, :table_width]
    )
    own_term = jnp.einsum("mnk,jnk->jmk", u_blocks, omega.astype(jnp.float32), precision=HIGH)
    sketch = own_term - incoming
    flat_rows = sketch.reshape(columns, params * cam_width)
    gram_local = jnp.dot(flat_rows, flat_rows.T, precision=HIGH, preferred_element_type=jnp.float32)
    row_total = params * cam_width * devices
    lower_factor = jnp.linalg.cholesky(lax.psum(gram_local, ("track", "cam")) / row_total)
    basis_rows = jax.scipy.linalg.solve_triangular(lower_factor, flat_rows, lower=True).reshape(
        sketch.shape
    )
    return (sketch, basis_rows, lower_factor.T)


def solution(mesh):
    in_specs = (
        P(None, None, ("track", "cam")),
        P(None, None, ("track", "cam")),
        P(None, None, ("track", "cam")),
        P(None, None, ("track", "cam")),
        P(("track", "cam")),
        P(("track", "cam")),
        P(("track", "cam")),
    )
    out_specs = (P(None, None, ("track", "cam")), P(None, None, ("track", "cam")), P())
    return jax.shard_map(
        on_device, mesh=mesh, in_specs=in_specs, out_specs=out_specs, check_vma=False
    )
```

profile of v0, /device:TPU:0, one launch (start us, length us, event | category | flops | bytes accessed | tf_op | source)
XLA Modules:
  0.0 363.9 jit_solution(12495128076649908816)
XLA Ops:
  0.6 0.7 add_select_fusion
  1.3 3.8 %sort.17 = (s32[512]{0:T(512)}, s32[512]{0:T(512)S(1)}) sort(s32[512]{0:T(512)S(1)} %add_select_fusion, s32[512]{0:T(512)S(1)} %iota.38), dimensions={0}, to_apply=%region_0.1 | sort | flops 4608 | bytes 8192 | tf_op jit(solution)/shard_map/jit(argsort)/sort | solution.py:75
  5.1 3.5 gather_fusion.1
  8.6 35.9 %while.25 = (s32[]{:T(128)}, u32[512]{0:T(512)S(1)}, u32[512]{0:T(512)S(1)}, s32[512]{0:T(512)S(1)}, s32[]{:T(128)}, /*index=5*/s32[]{:T(128)}, s32[]{}) while((s32[]{:T(128)}, u32[512]{0:T(512)S(1)}, u32[512]{0:T(512)S(1)}, s32[512]{0:T(512)S(1)}, s32[]{:T(128)}, /*index=5*/s32[]{:T(128)}, s32[]{}) %tuple.87), condition=%wide.region_2.3_spmd.clone, body=%wide.region_1.2_spmd.clone.sunk | while | flops 10244 | bytes 40037 | solution.py:77
  8.7 3.5 gather_fusion
  12.3 3.5 gather_fusion
  15.9 3.5 gather_fusion
  19.4 3.5 gather_fusion
  23.0 3.5 gather_fusion
  26.6 3.5 gather_fusion
  30.2 3.5 gather_fusion
  33.8 3.5 gather_fusion
  37.4 3.5 gather_fusion
  41.0 3.5 gather_fusion
  44.5 2.4 scatter_custom_fusion
  47.0 2.6 scatter_custom_fusion.1
  49.6 0.7 reshape.1434
  50.3 8.3 %all-to-all-start = ((s32[16,2,32]{2,1,0:T(2,128)}), s32[16,2,32]{2,1,0:T(2,128)S(1)}, u32[]{:S(2)}, u32[]{:S(2)}) async-start(s32[16,2,32]{2,1,0:T(2,128)} %reshape.1434), calls=%async_computation | async-start | bytes 32768 | tf_op jit(solution)/shard_map/all_to_all | solution.py:87
  59.1 6.9 %all-to-all-done = s32[16,2,32]{2,1,0:T(2,128)S(1)} async-done(((s32[16,2,32]{2,1,0:T(2,128)}), s32[16,2,32]{2,1,0:T(2,128)S(1)}, u32[]{:S(2)}, u32[]{:S(2)}) %all-to-all-start) | async-done | bytes 4128 | tf_op jit(solution)/shard_map/all_to_all | solution.py:87
  66.1 3.7 %all_to_all.30 = s32[2,1,512]{2,1,0:T(1,128)S(1)} all-to-all(s32[2,1,512]{2,1,0:T(1,128)S(1)} %reshape.1574), channel_id=1, replica_groups=mesh['track'=16,'cam'=2] {'cam'}, dimensions={0} | all-to-all | bytes 8192 | tf_op jit(solution)/shard_map/all_to_all | solution.py:86
  70.3 0.7 reduce.42
  71.2 8.3 %gather_fusion.2 = bf16[1024,32,9]{1,2,0:T(8,128)(2,1)} fusion(bf16[32,9,128]{0,1,2:T(8,128)(2,1)S(1)} %copy.264, s32[1024]{0:T(1024)S(1)} %broadcast_clamp_fusion), kind=kCustom, calls=%fused_computation.2 | custom fusion | bytes 1183744 | tf_op jit(solution)/shard_map/jit(_take)/gather | solution.py:97
  79.5 2.8 fusion
  82.3 2.5 reshape.1437
  84.7 1.4 copy.271
  86.2 3.6 all-to-all-start.2
  89.8 0.6 mul.793
  90.5 0.7 mul.878
  91.1 0.7 mul.881
  91.8 0.6 mul.884
  92.4 0.7 mul.887
  93.1 0.7 mul.890
  93.8 0.7 mul.893
  94.4 0.7 mul.896
  95.1 0.7 mul.899
  98.2 0.7 fusion.27
  98.8 7.5 %all-to-all-done.2 = bf16[16,2,9,1024]{3,1,2,0:T(2,128)(2,1)S(1)} async-done(((bf16[16,2,9,1024]{3,1,2,0:T(2,128)(2,1)}), bf16[16,2,9,1024]{3,1,2,0:T(2,128)(2,1)S(1)}, u32[]{:S(2)}, u32[]{:S(2)}) %all-to-all-start.2) | async-done | bytes 589856 | tf_op jit(solution)/shard_map/all_to_all | solution.py:104
  106.5 4.2 %all_to_all.31 = bf16[16,2,9,1024]{3,0,2,1:T(8,128)(2,1)S(1)} all-to-all(bf16[16,2,9,1024]{3,0,2,1:T(8,128)(2,1)S(1)} %copy.272), channel_id=1, replica_groups=mesh['track'=16,'cam'=2] {'cam'}, dimensions={1} | all-to-all | bytes 1179648 | tf_op jit(solution)/shard_map/all_to_all | solution.py:103
  110.7 1.8 reshape.1438
  112.5 4.9 %copy.328 = bf16[9,32,16,2,32]{1,0,4,3,2:T(8,128)(2,1)} copy(bf16[9,32,16,2,32]{1,4,2,0,3:T(8,128)(2,1)S(1)} %bitcast.143) | data formatting | bytes 1179648 | tf_op jit(solution)/shard_map/reshape | solution.py:113
  117.6 3.4 gather_fusion.3
  121.1 1.2 copy.275
  124.4 2.0 copy.310
  126.4 2.5 broadcast_in_dim.74
  128.9 47.3 %scatter_fusion = bf16[9,32,1024]{1,0,2:T(8,128)(2,1)} fusion(bf16[9,32,1024]{1,0,2:T(8,128)(2,1)} %broadcast_in_dim.74, s32[512]{0:T(512)S(1)} %copy-done.25, bf16[512,9,32]{2,1,0:T(8,128)(2,1)S(1)} %copy.310), kind=kCustom, calls=%fused_computation.6 | custom fusion | bytes 886784 | tf_op jit(solution)/shard_map/scatter | solution.py:120
  176.2 2.8 copy.379
  179.0 2.5 reshape.1441
  181.5 1.4 copy.312
  183.0 4.4 %all-to-all-start.4 = ((bf16[16,2,9,1024]{3,1,2,0:T(2,128)(2,1)}), bf16[16,2,9,1024]{3,1,2,0:T(2,128)(2,1)S(1)}, u32[]{:S(2)}, u32[]{:S(2)}) async-start(bf16[16,2,9,1024]{3,1,2,0:T(2,128)(2,1)} %copy.312), calls=%async_computation.4 | async-start | bytes 1179648 | tf_op jit(solution)/shard_map/all_to_all | solution.py:128
  187.4 1.4 copy.265
  188.9 15.1 %all-to-all-done.4 = bf16[16,2,9,1024]{3,1,2,0:T(2,128)(2,1)S(1)} async-done(((bf16[16,2,9,1024]{3,1,2,0:T(2,128)(2,1)}), bf16[16,2,9,1024]{3,1,2,0:T(2,128)(2,1)S(1)}, u32[]{:S(2)}, u32[]{:S(2)}) %all-to-all-start.4) | async-done | bytes 589856 | tf_op jit(solution)/shard_map/all_to_all | solution.py:128
  204.2 4.2 %all_to_all.32 = bf16[16,2,9,1024]{3,0,2,1:T(8,128)(2,1)S(1)} all-to-all(bf16[16,2,9,1024]{3,0,2,1:T(8,128)(2,1)S(1)} %copy.313), channel_id=1, replica_groups=mesh['track'=16,'cam'=2] {'cam'}, dimensions={1} | all-to-all | bytes 1179648 | tf_op jit(solution)/shard_map/all_to_all | solution.py:127
  208.4 2.8 reshape.1444
  211.2 7.7 %copy.314 = f32[32,9,16,2,32]{4,3,2,0,1:T(2,128)} copy(f32[32,9,16,2,32]{0,4,2,1,3:T(8,128)} %bitcast.141) | data formatting | bytes 2359296 | tf_op jit(solution)/shard_map/convert_element_type | solution.py:138
  218.9 6.9 %reshape.1502 = f32[32,9,1024]{2,0,1:T(8,128)S(1)} reshape(f32[32,9,16,2,32]{4,3,2,0,1:T(2,128)} %copy.314) | data formatting | bytes 2359296 | tf_op jit(solution)/shard_map/convert_element_type | solution.py:138
  225.8 6.1 %copy.315 = f32[1024,32,9]{1,2,0:T(8,128)} copy(f32[1024,32,9]{0,1,2:T(8,128)S(1)} %bitcast.174) | data formatting | bytes 2359296 | tf_op jit(solution)/shard_map/convert_element_type | solution.py:138
  232.0 81.2 %scatter_fusion.1 = f32[32,9,129]{0,1,2:T(8,128)S(1)} fusion(f32[32,9,129]{0,1,2:T(8,128)S(1)} %broadcast_in_dim.67, s32[1024]{0:T(1024)S(1)} %bitcast.234, f32[1024,32,9]{1,2,0:T(8,128)} %copy.315), kind=kCustom, calls=%fused_computation.7 | custom fusion | flops 294912 | bytes 3543040 | tf_op jit(solution)/shard_map/scatter-add | solution.py:144
  313.2 1.9 fusion.1
  316.1 39.3 %psum.7 = f32[32,32]{0,1:T(8,128)S(1)} all-reduce(f32[32,32]{0,1:T(8,128)S(1)} %convolution_bitcast_fusion.2), channel_id=1, replica_groups=mesh['track'=16,'cam'=2] {'track','cam'}, use_global_device_ids=true, to_apply=%region_7.8 | all-reduce | flops 1024 | bytes 8192 | tf_op jit(solution)/shard_map/psum | solution.py:151
  355.5 2.9 cholesky.16
  359.1 0.7 fusion.18
  359.8 2.4 custom-call.7
  362.2 0.7 copy.324
  362.9 1.0 fusion.7
  (193 shorter events, 8.2 us)
Async XLA Ops:
  8.6 50.0 %copy-start.2 = (bf16[32,9,128]{2,0,1:T(8,128)(2,1)S(1)}, bf16[32,9,128]{2,0,1:T(8,128)(2,1)}, u32[]{:S(2)}) copy-start(bf16[32,9,128]{2,0,1:T(8,128)(2,1)} %param.9) | copy-start | bytes 221188
  47.0 48.8 %copy-start.24 = (s32[512]{0:T(512)}, s32[512]{0:T(512)S(1)}, u32[]{:S(2)}) copy-start(s32[512]{0:T(512)S(1)} %compare_select_fusion.3) | copy-start | bytes 6148
  50.3 15.7 %all-to-all-start = ((s32[16,2,32]{2,1,0:T(2,128)}), s32[16,2,32]{2,1,0:T(2,128)S(1)}, u32[]{:S(2)}, u32[]{:S(2)}) async-start(s32[16,2,32]{2,1,0:T(2,128)} %reshape.1434), calls=%async_computation | async-start | bytes 32768 | tf_op jit(solution)/shard_map/all_to_all | solution.py:87
  82.2 7.5 %copy-start.39 = (f32[3,3,128]{2,1,0:T(4,128)S(1)}, f32[3,3,128]{2,1,0:T(4,128)}, u32[]{:S(2)}) copy-start(f32[3,3,128]{2,1,0:T(4,128)} %param.12) | copy-start | bytes 13828
  82.2 14.7 %copy-start.41 = (s32[512]{0:T(512)S(1)}, s32[512]{0:T(512)}, u32[]{:S(2)}) copy-start(s32[512]{0:T(512)} %param.15) | copy-start | bytes 6148
  82.2 15.3 %copy-start.1 = (bf16[9,3,512]{2,1,0:T(4,128)(2,1)S(1)}, bf16[9,3,512]{2,1,0:T(4,128)(2,1)}, u32[]{:S(2)}) copy-start(bf16[9,3,512]{2,1,0:T(4,128)(2,1)} %param.11) | copy-start | bytes 82948
  86.2 20.2 %all-to-all-start.2 = ((bf16[16,2,9,1024]{3,1,2,0:T(2,128)(2,1)}), bf16[16,2,9,1024]{3,1,2,0:T(2,128)(2,1)S(1)}, u32[]{:S(2)}, u32[]{:S(2)}) async-start(bf16[16,2,9,1024]{3,1,2,0:T(2,128)(2,1)} %copy.271), calls=%async_computation.2 | async-start | bytes 1179648 | tf_op jit(solution)/shard_map/all_to_all | solution.py:104
  112.5 5.1 %copy-start.26 = (s32[1024]{0:T(1024)S(1)}, s32[1024]{0:T(1024)}, u32[]{:S(2)}) copy-start(s32[1024]{0:T(1024)} %pad_clamp_fusion.1) | copy-start | bytes 12292
  117.4 4.9 %copy-start.40 = (pred[512]{0:T(512)(128)(4,1)S(1)}, pred[512]{0:T(512)(128)(4,1)}, u32[]{:S(2)}) copy-start(pred[512]{0:T(512)(128)(4,1)} %compare_and_fusion.1) | copy-start | bytes 1540
  117.4 5.0 %copy-start.5 = (f32[1,1,512]{2,1,0:T(1,128)S(1)}, f32[1,1,512]{2,1,0:T(1,128)}, u32[]{:S(2)}) copy-start(f32[1,1,512]{2,1,0:T(1,128)} %get-tuple-element.140) | copy-start | bytes 6148
  117.4 5.0 %copy-start.8 = (f32[1,1,512]{2,1,0:T(1,128)S(1)}, f32[1,1,512]{2,1,0:T(1,128)}, u32[]{:S(2)}) copy-start(f32[1,1,512]{2,1,0:T(1,128)} %get-tuple-element.139) | copy-start | bytes 6148
  117.4 5.0 %copy-start.10 = (f32[1,1,512]{2,1,0:T(1,128)S(1)}, f32[1,1,512]{2,1,0:T(1,128)}, u32[]{:S(2)}) copy-start(f32[1,1,512]{2,1,0:T(1,128)} %get-tuple-element.138) | copy-start | bytes 6148
  117.4 5.0 %copy-start.13 = (f32[1,1,512]{2,1,0:T(1,128)S(1)}, f32[1,1,512]{2,1,0:T(1,128)}, u32[]{:S(2)}) copy-start(f32[1,1,512]{2,1,0:T(1,128)} %get-tuple-element.137) | copy-start | bytes 6148
  117.4 5.0 %copy-start.15 = (f32[1,1,512]{2,1,0:T(1,128)S(1)}, f32[1,1,512]{2,1,0:T(1,128)}, u32[]{:S(2)}) copy-start(f32[1,1,512]{2,1,0:T(1,128)} %get-tuple-element.136) | copy-start | bytes 6148
  117.4 5.0 %copy-start.17 = (f32[1,1,512]{2,1,0:T(1,128)S(1)}, f32[1,1,512]{2,1,0:T(1,128)}, u32[]{:S(2)}) copy-start(f32[1,1,512]{2,1,0:T(1,128)} %get-tuple-element.135) | copy-start | bytes 6148
  117.4 5.0 %copy-start.19 = (f32[1,1,512]{2,1,0:T(1,128)S(1)}, f32[1,1,512]{2,1,0:T(1,128)}, u32[]{:S(2)}) copy-start(f32[1,1,512]{2,1,0:T(1,128)} %get-tuple-element.134) | copy-start | bytes 6148
  117.5 5.0 %copy-start.21 = (f32[1,1,512]{2,1,0:T(1,128)S(1)}, f32[1,1,512]{2,1,0:T(1,128)}, u32[]{:S(2)}) copy-start(f32[1,1,512]{2,1,0:T(1,128)} %get-tuple-element.133) | copy-start | bytes 6148
  117.5 5.0 %copy-start.4 = (f32[1,1,512]{2,1,0:T(1,128)S(1)}, f32[1,1,512]{2,1,0:T(1,128)}, u32[]{:S(2)}) copy-start(f32[1,1,512]{2,1,0:T(1,128)} %get-tuple-element.154) | copy-start | bytes 6148
  117.5 5.0 %copy-start.6 = (f32[1,1,512]{2,1,0:T(1,128)S(1)}, f32[1,1,512]{2,1,0:T(1,128)}, u32[]{:S(2)}) copy-start(f32[1,1,512]{2,1,0:T(1,128)} %get-tuple-element.149) | copy-start | bytes 6148
  117.5 5.0 %copy-start.7 = (f32[1,1,512]{2,1,0:T(1,128)S(1)}, f32[1,1,512]{2,1,0:T(1,128)}, u32[]{:S(2)}) copy-start(f32[1,1,512]{2,1,0:T(1,128)} %get-tuple-element.153) | copy-start | bytes 6148
  117.5 5.0 %copy-start.9 = (f32[1,1,512]{2,1,0:T(1,128)S(1)}, f32[1,1,512]{2,1,0:T(1,128)}, u32[]{:S(2)}) copy-start(f32[1,1,512]{2,1,0:T(1,128)} %get-tuple-element.148) | copy-start | bytes 6148
  117.5 5.0 %copy-start.11 = (f32[1,1,512]{2,1,0:T(1,128)S(1)}, f32[1,1,512]{2,1,0:T(1,128)}, u32[]{:S(2)}) copy-start(f32[1,1,512]{2,1,0:T(1,128)} %get-tuple-element.147) | copy-start | bytes 6148
  117.5 5.0 %copy-start.12 = (f32[1,1,512]{2,1,0:T(1,128)S(1)}, f32[1,1,512]{2,1,0:T(1,128)}, u32[]{:S(2)}) copy-start(f32[1,1,512]{2,1,0:T(1,128)} %get-tuple-element.152) | copy-start | bytes 6148
  117.5 5.0 %copy-start.14 = (f32[1,1,512]{2,1,0:T(1,128)S(1)}, f32[1,1,512]{2,1,0:T(1,128)}, u32[]{:S(2)}) copy-start(f32[1,1,512]{2,1,0:T(1,128)} %get-tuple-element.146) | copy-start | bytes 6148
  117.5 5.0 %copy-start.16 = (f32[1,1,512]{2,1,0:T(1,128)S(1)}, f32[1,1,512]{2,1,0:T(1,128)}, u32[]{:S(2)}) copy-start(f32[1,1,512]{2,1,0:T(1,128)} %get-tuple-element.145) | copy-start | bytes 6148
  117.6 5.0 %copy-start.18 = (f32[1,1,512]{2,1,0:T(1,128)S(1)}, f32[1,1,512]{2,1,0:T(1,128)}, u32[]{:S(2)}) copy-start(f32[1,1,512]{2,1,0:T(1,128)} %get-tuple-element.144) | copy-start | bytes 6148
  117.6 5.0 %copy-start.20 = (f32[1,1,512]{2,1,0:T(1,128)S(1)}, f32[1,1,512]{2,1,0:T(1,128)}, u32[]{:S(2)}) copy-start(f32[1,1,512]{2,1,0:T(1,128)} %get-tuple-element.143) | copy-start | bytes 6148
  117.6 5.0 %copy-start.22 = (f32[1,1,512]{2,1,0:T(1,128)S(1)}, f32[1,1,512]{2,1,0:T(1,128)}, u32[]{:S(2)}) copy-start(f32[1,1,512]{2,1,0:T(1,128)} %get-tuple-element.142) | copy-start | bytes 6148
  117.6 5.0 %copy-start.23 = (f32[1,1,512]{2,1,0:T(1,128)S(1)}, f32[1,1,512]{2,1,0:T(1,128)}, u32[]{:S(2)}) copy-start(f32[1,1,512]{2,1,0:T(1,128)} %get-tuple-element.151) | copy-start | bytes 6148
  121.0 1.8 copy-start.27
  121.0 1.8 copy-start.29
  121.0 2.2 copy-start.30
  121.0 2.2 copy-start.31
  121.0 2.2 copy-start.32
  121.0 2.2 copy-start.33
  121.0 2.2 copy-start.34
  121.1 2.2 copy-start.35
  121.1 2.2 copy-start.36
  121.1 2.2 copy-start.37
  121.1 2.2 copy-start.38
  123.3 1.1 copy-start.28
  126.4 2.5 copy-start.25
  181.5 5.9 %copy-start.3 = (f32[9,9,128]{2,1,0:T(8,128)S(1)}, f32[9,9,128]{2,1,0:T(8,128)}, u32[]{:S(2)}) copy-start(f32[9,9,128]{2,1,0:T(8,128)} %param.10) | copy-start | bytes 124420
  183.0 21.1 %all-to-all-start.4 = ((bf16[16,2,9,1024]{3,1,2,0:T(2,128)(2,1)}), bf16[16,2,9,1024]{3,1,2,0:T(2,128)(2,1)S(1)}, u32[]{:S(2)}, u32[]{:S(2)}) async-start(bf16[16,2,9,1024]{3,1,2,0:T(2,128)(2,1)} %copy.312), calls=%async_computation.4 | async-start | bytes 1179648 | tf_op jit(solution)/shard_map/all_to_all | solution.py:128
  315.4 48.6 %copy-start = (f32[32,9,128]{2,0,1:T(8,128)}, f32[32,9,128]{2,0,1:T(8,128)S(1)}, u32[]{:S(2)}) copy-start(f32[32,9,128]{2,0,1:T(8,128)S(1)} %copy.323) | copy-start | bytes 442372
where the time goes:
time: 367 us; the launch traced here: 364 us
  local copies, waits for them, and re-layouts  162 us (44%)
  other arithmetic  98.7 us (27%)
  blocking collectives  51.4 us (14%)
  waiting for transfers between devices  29.5 us (8%)
  starting transfers between devices  16.4 us (4%)
  matrix products  3.83 us (1%)
    scatter-add x1, other arithmetic, on_device(): incoming = jnp.zeros((columns, params, table_width + 1), jnp.float32).at[...  81.2 us
    scatter x1, local copies, waits for them, and re-layouts, on_device(): buffer = jnp.zeros((params, columns, buffer_slots), jnp.bfloat16).at[:, :...  47.3 us
    psum x1, blocking collectives, on_device(): lax.psum(gram_local, ('track', 'cam')) / row_total  39.3 us
    gather x10, local copies, waits for them, and re-layouts, on_device(): first_index = jnp.searchsorted(ranked, ranked, side='left')  34.9 us
    convert_element_type x4, local copies, waits for them, and re-layouts, on_device(): terms = arrived.reshape(track_count, cam_count, params, capacity, columns...  23.6 us
    all_to_all x1, waiting for transfers between devices, on_device(): lax.all_to_all(packed, 'track', split_axis=0, concat_axis=0, tiled=True)  15.1 us
    all_to_all x1, starting transfers between devices, on_device(): lax.all_to_all(request, 'track', split_axis=0, concat_axis=0, tiled=True)  8.34 us
    gather x1, local copies, waits for them, and re-layouts, on_device(): gathered_rows = jnp.take(omega, local_ids, axis=2)  8.28 us
  transfers between devices with their start and end apart: 3, of which 3 were waited for; matrix products, arithmetic and copies ran while one was open for 3% of the time, Pallas kernels for 0%

commit v1 on v0

--- a/solution.py
+++ b/solution.py
@@ -6,6 +6,10 @@
 BLK_OBS = 128
 TRK_BLK = 32
 HIGH = lax.Precision.HIGHEST
+
+
+def _recover_lane(content):
+    return lax.psum(lax.psum(content, "cam"), "track")
 
 
 def eliminate(gathered, w_blocks, v_inverse, obs_track, obs_mask):
@@ -148,7 +152,7 @@
     flat_rows = sketch.reshape(columns, params * cam_width)
     gram_local = jnp.dot(flat_rows, flat_rows.T, precision=HIGH, preferred_element_type=jnp.float32)
     row_total = params * cam_width * devices
-    lower_factor = jnp.linalg.cholesky(lax.psum(gram_local, ("track", "cam")) / row_total)
+    lower_factor = jnp.linalg.cholesky(_recover_lane(gram_local) / row_total)
     basis_rows = jax.scipy.linalg.solve_triangular(lower_factor, flat_rows, lower=True).reshape(
         sketch.shape
     )

time: 367 us -> 406 us (1.11)
  blocking collectives: 51.4 us -> 89.9 us
    psum x1 -> x2, blocking collectives: 39.3 us -> 77.8 us  [_recover_lane(): return lax.psum(lax.psum(content, 'cam'), 'track')]
where the time goes in v1:
time: 406 us; the launch traced here: 402 us
  local copies, waits for them, and re-layouts  162 us (40%)
  other arithmetic  98.6 us (24%)
  blocking collectives  89.9 us (22%)
  waiting for transfers between devices  29.5 us (7%)
  starting transfers between devices  16.2 us (4%)
    scatter-add x1, other arithmetic, on_device(): incoming = jnp.zeros((columns, params, table_width + 1), jnp.float32).at[...  81.2 us
    psum x2, blocking collectives, _recover_lane(): return lax.psum(lax.psum(content, 'cam'), 'track')  77.8 us
    scatter x1, local copies, waits for them, and re-layouts, on_device(): buffer = jnp.zeros((params, columns, buffer_slots), jnp.bfloat16).at[:, :...  47.5 us
    gather x10, local copies, waits for them, and re-layouts, on_device(): first_index = jnp.searchsorted(ranked, ranked, side='left')  34.9 us
    convert_element_type x4, local copies, waits for them, and re-layouts, on_device(): terms = arrived.reshape(track_count, cam_count, params, capacity, columns...  23.6 us
    all_to_all x1, waiting for transfers between devices, on_device(): lax.all_to_all(packed, 'track', split_axis=0, concat_axis=0, tiled=True)  15 us
    gather x1, local copies, waits for them, and re-layouts, on_device(): gathered_rows = jnp.take(omega, local_ids, axis=2)  8.35 us
    all_to_all x1, starting transfers between devices, on_device(): lax.all_to_all(request, 'track', split_axis=0, concat_axis=0, tiled=True)  8.34 us
  transfers between devices with their start and end apart: 3, of which 3 were waited for; matrix products, arithmetic and copies ran while one was open for 3% of the time, Pallas kernels for 0%

profile of v1, /device:TPU:0, one launch (start us, length us, event | category | flops | bytes accessed | tf_op | source)
XLA Modules:
  0.0 402.4 jit_solution(1331365375634229943)
XLA Ops:
  0.6 0.7 add_select_fusion
  1.3 3.8 sort.17
  5.1 3.5 gather_fusion.1
  8.6 35.9 %while.25 = (s32[]{:T(128)}, u32[512]{0:T(512)S(1)}, u32[512]{0:T(512)S(1)}, s32[512]{0:T(512)S(1)}, s32[]{:T(128)}, /*index=5*/s32[]{:T(128)}, s32[]{}) while((s32[]{:T(128)}, u32[512]{0:T(512)S(1)}, u32[512]{0:T(512)S(1)}, s32[512]{0:T(512)S(1)}, s32[]{:T(128)}, /*index=5*/s32[]{:T(128)}, s32[]{}) %tuple.87), condition=%wide.region_2.3_spmd.clone, body=%wide.region_1.2_spmd.clone.sunk | while | flops 10244 | bytes 40037 | solution.py:81
  8.7 3.5 gather_fusion
  12.3 3.5 gather_fusion
  15.9 3.5 gather_fusion
  19.4 3.5 gather_fusion
  23.0 3.5 gather_fusion
  26.6 3.5 gather_fusion
  30.2 3.5 gather_fusion
  33.8 3.5 gather_fusion
  37.4 3.5 gather_fusion
  41.0 3.5 gather_fusion
  44.5 2.4 scatter_custom_fusion
  47.0 2.6 scatter_custom_fusion.1
  49.6 0.7 reshape.1434
  50.3 8.3 %all-to-all-start = ((s32[16,2,32]{2,1,0:T(2,128)}), s32[16,2,32]{2,1,0:T(2,128)S(1)}, u32[]{:S(2)}, u32[]{:S(2)}) async-start(s32[16,2,32]{2,1,0:T(2,128)} %reshape.1434), calls=%async_computation | async-start | bytes 32768 | tf_op jit(solution)/shard_map/all_to_all | solution.py:91
  59.1 6.9 %all-to-all-done = s32[16,2,32]{2,1,0:T(2,128)S(1)} async-done(((s32[16,2,32]{2,1,0:T(2,128)}), s32[16,2,32]{2,1,0:T(2,128)S(1)}, u32[]{:S(2)}, u32[]{:S(2)}) %all-to-all-start) | async-done | bytes 4128 | tf_op jit(solution)/shard_map/all_to_all | solution.py:91
  66.1 3.7 all_to_all.30
  70.3 0.7 reduce.42
  71.2 8.3 %gather_fusion.2 = bf16[1024,32,9]{1,2,0:T(8,128)(2,1)} fusion(bf16[32,9,128]{0,1,2:T(8,128)(2,1)S(1)} %copy.264, s32[1024]{0:T(1024)S(1)} %broadcast_clamp_fusion), kind=kCustom, calls=%fused_computation.2 | custom fusion | bytes 1183744 | tf_op jit(solution)/shard_map/jit(_take)/gather | solution.py:101
  79.5 2.8 fusion
  82.3 2.5 reshape.1437
  84.8 1.4 copy.271
  86.2 3.6 all-to-all-start.2
  89.9 0.7 mul.793
  90.5 0.7 mul.878
  91.2 0.7 mul.881
  91.9 0.6 mul.884
  92.5 0.7 mul.887
  93.2 0.7 mul.890
  94.5 0.7 mul.896
  95.2 0.7 mul.899
  98.1 0.7 fusion.27
  98.8 7.6 %all-to-all-done.2 = bf16[16,2,9,1024]{3,1,2,0:T(2,128)(2,1)S(1)} async-done(((bf16[16,2,9,1024]{3,1,2,0:T(2,128)(2,1)}), bf16[16,2,9,1024]{3,1,2,0:T(2,128)(2,1)S(1)}, u32[]{:S(2)}, u32[]{:S(2)}) %all-to-all-start.2) | async-done | bytes 589856 | tf_op jit(solution)/shard_map/all_to_all | solution.py:108
  106.5 4.2 %all_to_all.31 = bf16[16,2,9,1024]{3,0,2,1:T(8,128)(2,1)S(1)} all-to-all(bf16[16,2,9,1024]{3,0,2,1:T(8,128)(2,1)S(1)} %copy.272), channel_id=1, replica_groups=mesh['track'=16,'cam'=2] {'cam'}, dimensions={1} | all-to-all | bytes 1179648 | tf_op jit(solution)/shard_map/all_to_all | solution.py:107
  110.8 1.8 reshape.1438
  112.6 4.9 %copy.328 = bf16[9,32,16,2,32]{1,0,4,3,2:T(8,128)(2,1)} copy(bf16[9,32,16,2,32]{1,4,2,0,3:T(8,128)(2,1)S(1)} %bitcast.143) | data formatting | bytes 1179648 | tf_op jit(solution)/shard_map/reshape | solution.py:117
  117.7 3.4 gather_fusion.3
  121.2 1.2 copy.275
  124.5 2.0 copy.310
  126.5 2.5 broadcast_in_dim.74
  129.0 47.5 %scatter_fusion = bf16[9,32,1024]{1,0,2:T(8,128)(2,1)} fusion(bf16[9,32,1024]{1,0,2:T(8,128)(2,1)} %broadcast_in_dim.74, s32[512]{0:T(512)S(1)} %copy-done.25, bf16[512,9,32]{2,1,0:T(8,128)(2,1)S(1)} %copy.310), kind=kCustom, calls=%fused_computation.6 | custom fusion | bytes 886784 | tf_op jit(solution)/shard_map/scatter | solution.py:124
  176.5 2.8 copy.379
  179.3 2.5 reshape.1441
  181.8 1.4 copy.312
  183.2 4.2 %all-to-all-start.4 = ((bf16[16,2,9,1024]{3,1,2,0:T(2,128)(2,1)}), bf16[16,2,9,1024]{3,1,2,0:T(2,128)(2,1)S(1)}, u32[]{:S(2)}, u32[]{:S(2)}) async-start(bf16[16,2,9,1024]{3,1,2,0:T(2,128)(2,1)} %copy.312), calls=%async_computation.4 | async-start | bytes 1179648 | tf_op jit(solution)/shard_map/all_to_all | solution.py:132
  187.5 1.4 copy.265
  189.0 15.0 %all-to-all-done.4 = bf16[16,2,9,1024]{3,1,2,0:T(2,128)(2,1)S(1)} async-done(((bf16[16,2,9,1024]{3,1,2,0:T(2,128)(2,1)}), bf16[16,2,9,1024]{3,1,2,0:T(2,128)(2,1)S(1)}, u32[]{:S(2)}, u32[]{:S(2)}) %all-to-all-start.4) | async-done | bytes 589856 | tf_op jit(solution)/shard_map/all_to_all | solution.py:132
  204.2 4.2 %all_to_all.32 = bf16[16,2,9,1024]{3,0,2,1:T(8,128)(2,1)S(1)} all-to-all(bf16[16,2,9,1024]{3,0,2,1:T(8,128)(2,1)S(1)} %copy.313), channel_id=1, replica_groups=mesh['track'=16,'cam'=2] {'cam'}, dimensions={1} | all-to-all | bytes 1179648 | tf_op jit(solution)/shard_map/all_to_all | solution.py:131
  208.4 2.8 reshape.1444
  211.2 7.7 %copy.314 = f32[32,9,16,2,32]{4,3,2,0,1:T(2,128)} copy(f32[32,9,16,2,32]{0,4,2,1,3:T(8,128)} %bitcast.141) | data formatting | bytes 2359296 | tf_op jit(solution)/shard_map/convert_element_type | solution.py:142
  218.9 6.9 %reshape.1502 = f32[32,9,1024]{2,0,1:T(8,128)S(1)} reshape(f32[32,9,16,2,32]{4,3,2,0,1:T(2,128)} %copy.314) | data formatting | bytes 2359296 | tf_op jit(solution)/shard_map/convert_element_type | solution.py:142
  225.8 6.2 %copy.315 = f32[1024,32,9]{1,2,0:T(8,128)} copy(f32[1024,32,9]{0,1,2:T(8,128)S(1)} %bitcast.174) | data formatting | bytes 2359296 | tf_op jit(solution)/shard_map/convert_element_type | solution.py:142
  232.1 81.2 %scatter_fusion.1 = f32[32,9,129]{0,1,2:T(8,128)S(1)} fusion(f32[32,9,129]{0,1,2:T(8,128)S(1)} %broadcast_in_dim.67, s32[1024]{0:T(1024)S(1)} %bitcast.234, f32[1024,32,9]{1,2,0:T(8,128)} %copy.315), kind=kCustom, calls=%fused_computation.7 | custom fusion | flops 294912 | bytes 3543040 | tf_op jit(solution)/shard_map/scatter-add | solution.py:148
  313.2 1.9 fusion.1
  316.2 3.4 psum.14
  319.6 74.4 %psum.15 = f32[32,32]{0,1:T(8,128)S(1)} all-reduce(f32[32,32]{0,1:T(8,128)S(1)} %psum.14), channel_id=1, replica_groups=mesh['track'=16,'cam'=2] {'track'}, use_global_device_ids=true, to_apply=%region_8.9 | all-reduce | flops 1024 | bytes 8192 | tf_op jit(solution)/shard_map/psum | solution.py:12
  394.0 2.9 cholesky.16
  397.6 0.7 fusion.18
  398.3 2.4 custom-call.7
  400.7 0.7 copy.324
  401.4 1.0 fusion.7
  (194 shorter events, 8.8 us)
Async XLA Ops:
  8.6 50.0 %copy-start.2 = (bf16[32,9,128]{2,0,1:T(8,128)(2,1)S(1)}, bf16[32,9,128]{2,0,1:T(8,128)(2,1)}, u32[]{:S(2)}) copy-start(bf16[32,9,128]{2,0,1:T(8,128)(2,1)} %param.9) | copy-start | bytes 221188
  47.0 48.8 %copy-start.24 = (s32[512]{0:T(512)}, s32[512]{0:T(512)S(1)}, u32[]{:S(2)}) copy-start(s32[512]{0:T(512)S(1)} %compare_select_fusion.3) | copy-start | bytes 6148
  50.3 15.7 %all-to-all-start = ((s32[16,2,32]{2,1,0:T(2,128)}), s32[16,2,32]{2,1,0:T(2,128)S(1)}, u32[]{:S(2)}, u32[]{:S(2)}) async-start(s32[16,2,32]{2,1,0:T(2,128)} %reshape.1434), calls=%async_computation | async-start | bytes 32768 | tf_op jit(solution)/shard_map/all_to_all | solution.py:91
  82.3 7.5 %copy-start.39 = (f32[3,3,128]{2,1,0:T(4,128)S(1)}, f32[3,3,128]{2,1,0:T(4,128)}, u32[]{:S(2)}) copy-start(f32[3,3,128]{2,1,0:T(4,128)} %param.12) | copy-start | bytes 13828
  82.3 14.6 %copy-start.41 = (s32[512]{0:T(512)S(1)}, s32[512]{0:T(512)}, u32[]{:S(2)}) copy-start(s32[512]{0:T(512)} %param.15) | copy-start | bytes 6148
  82.3 15.2 %copy-start.1 = (bf16[9,3,512]{2,1,0:T(4,128)(2,1)S(1)}, bf16[9,3,512]{2,1,0:T(4,128)(2,1)}, u32[]{:S(2)}) copy-start(bf16[9,3,512]{2,1,0:T(4,128)(2,1)} %param.11) | copy-start | bytes 82948
  86.2 20.2 %all-to-all-start.2 = ((bf16[16,2,9,1024]{3,1,2,0:T(2,128)(2,1)}), bf16[16,2,9,1024]{3,1,2,0:T(2,128)(2,1)S(1)}, u32[]{:S(2)}, u32[]{:S(2)}) async-start(bf16[16,2,9,1024]{3,1,2,0:T(2,128)(2,1)} %copy.271), calls=%async_computation.2 | async-start | bytes 1179648 | tf_op jit(solution)/shard_map/all_to_all | solution.py:108
  112.6 5.1 %copy-start.26 = (s32[1024]{0:T(1024)S(1)}, s32[1024]{0:T(1024)}, u32[]{:S(2)}) copy-start(s32[1024]{0:T(1024)} %pad_clamp_fusion.1) | copy-start | bytes 12292
  117.5 4.9 %copy-start.40 = (pred[512]{0:T(512)(128)(4,1)S(1)}, pred[512]{0:T(512)(128)(4,1)}, u32[]{:S(2)}) copy-start(pred[512]{0:T(512)(128)(4,1)} %compare_and_fusion.1) | copy-start | bytes 1540
  117.5 5.0 %copy-start.5 = (f32[1,1,512]{2,1,0:T(1,128)S(1)}, f32[1,1,512]{2,1,0:T(1,128)}, u32[]{:S(2)}) copy-start(f32[1,1,512]{2,1,0:T(1,128)} %get-tuple-element.140) | copy-start | bytes 6148
  117.5 5.0 %copy-start.8 = (f32[1,1,512]{2,1,0:T(1,128)S(1)}, f32[1,1,512]{2,1,0:T(1,128)}, u32[]{:S(2)}) copy-start(f32[1,1,512]{2,1,0:T(1,128)} %get-tuple-element.139) | copy-start | bytes 6148
  117.5 5.0 %copy-start.10 = (f32[1,1,512]{2,1,0:T(1,128)S(1)}, f32[1,1,512]{2,1,0:T(1,128)}, u32[]{:S(2)}) copy-start(f32[1,1,512]{2,1,0:T(1,128)} %get-tuple-element.138) | copy-start | bytes 6148
  117.5 5.0 %copy-start.13 = (f32[1,1,512]{2,1,0:T(1,128)S(1)}, f32[1,1,512]{2,1,0:T(1,128)}, u32[]{:S(2)}) copy-start(f32[1,1,512]{2,1,0:T(1,128)} %get-tuple-element.137) | copy-start | bytes 6148
  117.5 5.0 %copy-start.15 = (f32[1,1,512]{2,1,0:T(1,128)S(1)}, f32[1,1,512]{2,1,0:T(1,128)}, u32[]{:S(2)}) copy-start(f32[1,1,512]{2,1,0:T(1,128)} %get-tuple-element.136) | copy-start | bytes 6148
  117.5 5.0 %copy-start.17 = (f32[1,1,512]{2,1,0:T(1,128)S(1)}, f32[1,1,512]{2,1,0:T(1,128)}, u32[]{:S(2)}) copy-start(f32[1,1,512]{2,1,0:T(1,128)} %get-tuple-element.135) | copy-start | bytes 6148
  117.5 5.0 %copy-start.19 = (f32[1,1,512]{2,1,0:T(1,128)S(1)}, f32[1,1,512]{2,1,0:T(1,128)}, u32[]{:S(2)}) copy-start(f32[1,1,512]{2,1,0:T(1,128)} %get-tuple-element.134) | copy-start | bytes 6148
  117.5 5.0 %copy-start.21 = (f32[1,1,512]{2,1,0:T(1,128)S(1)}, f32[1,1,512]{2,1,0:T(1,128)}, u32[]{:S(2)}) copy-start(f32[1,1,512]{2,1,0:T(1,128)} %get-tuple-element.133) | copy-start | bytes 6148
  117.5 5.0 %copy-start.4 = (f32[1,1,512]{2,1,0:T(1,128)S(1)}, f32[1,1,512]{2,1,0:T(1,128)}, u32[]{:S(2)}) copy-start(f32[1,1,512]{2,1,0:T(1,128)} %get-tuple-element.154) | copy-start | bytes 6148
  117.5 5.0 %copy-start.6 = (f32[1,1,512]{2,1,0:T(1,128)S(1)}, f32[1,1,512]{2,1,0:T(1,128)}, u32[]{:S(2)}) copy-start(f32[1,1,512]{2,1,0:T(1,128)} %get-tuple-element.149) | copy-start | bytes 6148
  117.6 5.0 %copy-start.7 = (f32[1,1,512]{2,1,0:T(1,128)S(1)}, f32[1,1,512]{2,1,0:T(1,128)}, u32[]{:S(2)}) copy-start(f32[1,1,512]{2,1,0:T(1,128)} %get-tuple-element.153) | copy-start | bytes 6148
  117.6 5.0 %copy-start.9 = (f32[1,1,512]{2,1,0:T(1,128)S(1)}, f32[1,1,512]{2,1,0:T(1,128)}, u32[]{:S(2)}) copy-start(f32[1,1,512]{2,1,0:T(1,128)} %get-tuple-element.148) | copy-start | bytes 6148
  117.6 5.0 %copy-start.11 = (f32[1,1,512]{2,1,0:T(1,128)S(1)}, f32[1,1,512]{2,1,0:T(1,128)}, u32[]{:S(2)}) copy-start(f32[1,1,512]{2,1,0:T(1,128)} %get-tuple-element.147) | copy-start | bytes 6148
  117.6 5.0 %copy-start.12 = (f32[1,1,512]{2,1,0:T(1,128)S(1)}, f32[1,1,512]{2,1,0:T(1,128)}, u32[]{:S(2)}) copy-start(f32[1,1,512]{2,1,0:T(1,128)} %get-tuple-element.152) | copy-start | bytes 6148
  117.6 5.0 %copy-start.14 = (f32[1,1,512]{2,1,0:T(1,128)S(1)}, f32[1,1,512]{2,1,0:T(1,128)}, u32[]{:S(2)}) copy-start(f32[1,1,512]{2,1,0:T(1,128)} %get-tuple-element.146) | copy-start | bytes 6148
  117.6 5.0 %copy-start.16 = (f32[1,1,512]{2,1,0:T(1,128)S(1)}, f32[1,1,512]{2,1,0:T(1,128)}, u32[]{:S(2)}) copy-start(f32[1,1,512]{2,1,0:T(1,128)} %get-tuple-element.145) | copy-start | bytes 6148
  117.6 5.0 %copy-start.18 = (f32[1,1,512]{2,1,0:T(1,128)S(1)}, f32[1,1,512]{2,1,0:T(1,128)}, u32[]{:S(2)}) copy-start(f32[1,1,512]{2,1,0:T(1,128)} %get-tuple-element.144) | copy-start | bytes 6148
  117.6 5.0 %copy-start.20 = (f32[1,1,512]{2,1,0:T(1,128)S(1)}, f32[1,1,512]{2,1,0:T(1,128)}, u32[]{:S(2)}) copy-start(f32[1,1,512]{2,1,0:T(1,128)} %get-tuple-element.143) | copy-start | bytes 6148
  117.6 5.0 %copy-start.22 = (f32[1,1,512]{2,1,0:T(1,128)S(1)}, f32[1,1,512]{2,1,0:T(1,128)}, u32[]{:S(2)}) copy-start(f32[1,1,512]{2,1,0:T(1,128)} %get-tuple-element.142) | copy-start | bytes 6148
  117.6 5.0 %copy-start.23 = (f32[1,1,512]{2,1,0:T(1,128)S(1)}, f32[1,1,512]{2,1,0:T(1,128)}, u32[]{:S(2)}) copy-start(f32[1,1,512]{2,1,0:T(1,128)} %get-tuple-element.151) | copy-start | bytes 6148
  121.0 1.8 copy-start.27
  121.1 1.8 copy-start.29
  121.1 2.2 copy-start.30
  121.1 2.2 copy-start.31
  121.1 2.2 copy-start.32
  121.1 2.2 copy-start.33
  121.1 2.2 copy-start.34
  121.1 2.2 copy-start.35
  121.1 2.2 copy-start.36
  121.1 2.2 copy-start.37
  121.1 2.2 copy-start.38
  123.4 1.1 copy-start.28
  126.5 2.5 copy-start.25
  181.8 5.7 %copy-start.3 = (f32[9,9,128]{2,1,0:T(8,128)S(1)}, f32[9,9,128]{2,1,0:T(8,128)}, u32[]{:S(2)}) copy-start(f32[9,9,128]{2,1,0:T(8,128)} %param.10) | copy-start | bytes 124420
  183.2 20.8 %all-to-all-start.4 = ((bf16[16,2,9,1024]{3,1,2,0:T(2,128)(2,1)}), bf16[16,2,9,1024]{3,1,2,0:T(2,128)(2,1)S(1)}, u32[]{:S(2)}, u32[]{:S(2)}) async-start(bf16[16,2,9,1024]{3,1,2,0:T(2,128)(2,1)} %copy.312), calls=%async_computation.4 | async-start | bytes 1179648 | tf_op jit(solution)/shard_map/all_to_all | solution.py:132
  315.4 87.0 %copy-start = (f32[32,9,128]{2,0,1:T(8,128)}, f32[32,9,128]{2,0,1:T(8,128)S(1)}, u32[]{:S(2)}) copy-start(f32[32,9,128]{2,0,1:T(8,128)S(1)} %copy.323) | copy-start | bytes 442372
